TPU v7x, 32 devices: a whole 2x2x4 slice. The times are simulated.
32 devices in a mesh: leaf: 8 (over z, x), vec: 4 (over y, core).
Axes of the slice: x: 2, y: 2, z: 4, core: 2. Of those that a mesh axis runs over, the one named last changes fastest.
Arguments:
- samples: bfloat16 [64, 32768], P('vec', 'leaf'), may hold values from -6 to 6
- coords: float32 [3, 32768], P(None, 'leaf'), may hold values from -4 to 4
- panel_area: float32 [32768], P('leaf'), may hold values from 0.05 to 0.5
- quad_weight: float32 [32768], P('leaf'), may hold values from 0.2 to 1
- leaf_basis: bfloat16 [128, 64, 256], P('leaf'), may hold values from -0.375 to 0.375
- transfer: bfloat16 [64, 2, 64, 64], P('leaf'), may hold values from -0.5 to 0.5
- coupling_fine: bfloat16 [128, 16, 64, 64], P('leaf'), may hold values from -0.1875 to 0.1875
- coupling_coarse: bfloat16 [64, 16, 64, 64], P('leaf'), may hold values from -0.1875 to 0.1875
- near_list: int32 [128, 16], P('leaf'), may hold values from 0 to 127, as said below
- send_fine: int32 [64, 32], P('leaf'), may hold values from 0 to 15
- send_coarse: int32 [64, 16], P('leaf'), may hold values from 0 to 7
- far_fine: int32 [128, 16], P('leaf'), may hold values from 0 to 255, as said below
- far_coarse: int32 [64, 16], P('leaf'), may hold values from 0 to 127, as said below
Outputs:
- sample_out: bfloat16 [64, 32768], P('vec', 'leaf')
- sample_gram: float32 [128, 64, 64], P('leaf', 'vec')
Inputs may be any that keep to these rules, and one draw needn't show every extreme that they name: `near_list`: row g names 16 different leaves, each at most 16 leaves from g. `send_fine`: row e * 8 + d names clusters of device e, counted on e from 0; every slot carries one. `send_coarse`: row e * 8 + d names clusters of device e, counted on e from 0; every slot carries one. `far_fine`: the rows of one device's 16 leaves name each of the values 0 to 255 exactly once. `far_coarse`: the rows of one device's parents name each of the values 0 to 127 exactly once.
All inputs are finite; a program needn't handle non-finite values.
Results may differ from a plain program's by a relative error of at most 0.0085.
Values may be sent and summed in bfloat16 or wider, within the bound.
A program may use at most 64 MiB of HBM per device.

v0:
```python
import jax
import jax.numpy as jnp
from jax import lax
from jax.sharding import PartitionSpec as P

LEAF = 256
HW = 16


four_pi = 4.0 * 3.141592653589793


def extended(block, sides, width):
    for axis, dim in sides:
        count = lax.axis_size(axis)
        forward = [(i, i + 1) for i in range(count - 1)]
        backward = [(target, source) for source, target in forward]
        low = lax.ppermute(
            lax.slice_in_dim(block, block.shape[dim] - width, None, axis=dim), axis, forward
        )
        high = lax.ppermute(lax.slice_in_dim(block, 0, width, axis=dim), axis, backward)
        block = jnp.concatenate([low, block, high], axis=dim)
    return block


def kernel_block(target, source):
    delta_x = target[0][:, None] - source[0][None, :]
    delta_y = target[1][:, None] - source[1][None, :]
    delta_z = target[2][:, None] - source[2][None, :]
    distance = delta_x * delta_x + delta_y * delta_y + delta_z * delta_z + source[3][None, :]
    return (source[4][None, :] / (four_pi * jnp.sqrt(distance))).astype(jnp.bfloat16)


def apply_coupling(tile_set, received, far_list, vec_dev, basis_rank):
    coef_table = received.reshape(-1, vec_dev, basis_rank)
    picked = coef_table[far_list]
    return jnp.einsum("ibkl,ibvl->ivk", tile_set, picked, preferred_element_type=jnp.float32)


def near_leaves(leaf_ids, window, geo_leaves, vec_leaves, targets):

    def one_leaf(index):
        chosen = window[index]
        src_geo = jnp.take(geo_leaves, chosen, axis=1)
        src_vec = jnp.take(vec_leaves, chosen, axis=1)
        target = lax.dynamic_index_in_dim(targets, index, 1, keepdims=False)
        blocks = jax.vmap(kernel_block, (None, 1))(target, src_geo)
        return jnp.einsum("npq,vnq->vp", blocks, src_vec, preferred_element_type=jnp.float32)

    return lax.map(one_leaf, leaf_ids)


def per_device(
    samples,
    coords,
    panel_area,
    quad_weight,
    leaf_basis,
    transfer,
    coupling_fine,
    coupling_coarse,
    near_list,
    send_fine,
    send_coarse,
    far_fine,
    far_coarse,
):
    vec_dev, points = samples.shape
    leaf_dev, basis_rank, leaf_pts = leaf_basis.shape
    devices = lax.axis_size("leaf")
    device = lax.axis_index("leaf")
    geometry = jnp.concatenate([coords, panel_area[None, :], quad_weight[None, :]], axis=0)
    geo_wide = extended(geometry, (("leaf", 1),), HW * leaf_pts)
    vec_wide = extended(samples, (("leaf", 1),), HW * leaf_pts)
    geo_leaves = geo_wide.reshape(5, -1, leaf_pts)
    window = near_list - (device * leaf_dev - HW)
    targets = coords.reshape(3, leaf_dev, leaf_pts)
    local_rows = samples.reshape(vec_dev, leaf_dev, leaf_pts)
    fine_coef = jnp.einsum(
        "ikp,vip->ivk", leaf_basis, local_rows, preferred_element_type=jnp.float32
    ).astype(jnp.bfloat16)
    coarse_coef = jnp.einsum(
        "mskl,msvk->mvl",
        transfer,
        fine_coef.reshape(-1, 2, vec_dev, basis_rank),
        preferred_element_type=jnp.float32,
    ).astype(jnp.bfloat16)
    send_leafs = fine_coef[send_fine].reshape(devices, -1, vec_dev * basis_rank)
    send_parents = coarse_coef[send_coarse].reshape(devices, -1, vec_dev * basis_rank)
    got_leafs = lax.all_to_all(send_leafs, "leaf", split_axis=0, concat_axis=0, tiled=True)
    got_parents = lax.all_to_all(send_parents, "leaf", split_axis=0, concat_axis=0, tiled=True)
    vec_groups = lax.axis_size("vec")
    quarter = leaf_dev // vec_groups
    all_wide = lax.all_gather(vec_wide, "vec", axis=0, tiled=True)
    all_leaves = all_wide.reshape(all_wide.shape[0], -1, leaf_pts)
    first_leaf = lax.axis_index("vec") * quarter
    leaf_ids = first_leaf + jnp.arange(quarter, dtype=jnp.int32)
    near_quarter = near_leaves(leaf_ids, window, geo_leaves, all_leaves, targets)
    near_part = lax.all_to_all(
        near_quarter.astype(jnp.bfloat16), "vec", split_axis=1, concat_axis=0, tiled=True
    ).astype(near_quarter.dtype)
    field_fine = apply_coupling(coupling_fine, got_leafs, far_fine, vec_dev, basis_rank)
    field_coarse = apply_coupling(
        coupling_coarse, got_parents, far_coarse, vec_dev, basis_rank
    ).astype(jnp.bfloat16)
    pushed = jnp.einsum(
        "mskl,mvl->msvk", transfer, field_coarse, preferred_element_type=jnp.float32
    )
    local_field = (field_fine + pushed.reshape(leaf_dev, vec_dev, basis_rank)).astype(jnp.bfloat16)
    far_part = jnp.einsum(
        "ikp,ivk->vip", leaf_basis, local_field, preferred_element_type=jnp.float32
    )
    sample_out = (
        (jnp.transpose(near_part, (1, 0, 2)) + far_part)
        .reshape(vec_dev, points)
        .astype(jnp.bfloat16)
    )
    own_rows = sample_out.reshape(vec_dev, leaf_dev, leaf_pts)
    shard_rows = lax.all_gather(sample_out, "vec", axis=0, tiled=True)
    shaped = shard_rows.reshape(shard_rows.shape[0], leaf_dev, leaf_pts)
    sample_gram = jnp.einsum(
        "vip,wip->ivw", own_rows, shaped, preferred_element_type=jnp.float32
    ) * (1.0 / LEAF)
    return (sample_out, sample_gram)


def solution(mesh):
    return jax.shard_map(
        per_device,
        mesh=mesh,
        in_specs=(
            P("vec", "leaf"),
            P(None, "leaf"),
            P("leaf"),
            P("leaf"),
            P("leaf", None, None),
            P("leaf", None, None, None),
            P("leaf", None, None, None),
            P("leaf", None, None, None),
            P("leaf", None),
            P("leaf", None),
            P("leaf", None),
            P("leaf", None),
            P("leaf", None),
        ),
        out_specs=(P("vec", "leaf"), P("leaf", "vec", None)),
        check_vma=False,
    )
```

profile of v0, /device:TPU:0, one launch (start us, length us, event | category | flops | bytes accessed | tf_op | source)
XLA Modules:
  0.0 151.8 jit_solution(12427839923435013858)
XLA Ops:
  7.2 1.4 collective-permute-start.1
  8.6 5.5 %collective-permute-start = (bf16[16,4096]{1,0:T(8,128)(2,1)}, bf16[16,4096]{1,0:T(8,128)(2,1)S(1)}, u32[]{:S(2)}, u32[]{:S(2)}) collective-permute-start(bf16[16,4096]{1,0:T(8,128)(2,1)} %param.15), channel_id=1, source_target_pairs={{0,4},{4,8},{8,12},{12,16},{16,20},{20,24},{24,28},{1,5},{5,9},{9,... | collective-permute-start | bytes 393224 | tf_op jit(solution)/shard_map/ppermute | solution.py:18
  14.2 0.9 pad_maximum_fusion.2
  15.1 1.3 collective-permute-start.3
  16.4 6.1 %collective-permute-start.2 = (f32[5,4096]{1,0:T(8,128)S(1)}, f32[5,4096]{1,0:T(8,128)}, u32[]{:S(2)}, u32[]{:S(2)}) collective-permute-start(f32[5,4096]{1,0:T(8,128)S(1)} %pad_maximum_fusion.2), channel_id=1, source_target_pairs={{0,4},{4,8},{8,12},{12,16},{16,20},{20,24},{24,28},{1,5},{5,9},{9,... | collective-permute-start | bytes 245768 | tf_op jit(solution)/shard_map/ppermute | solution.py:18
  23.3 1.4 convolution_convert_fusion
  24.6 1.2 fusion.12
  25.9 0.7 gather_fusion.4
  26.6 1.0 reshape.99
  27.6 5.6 %all-to-all-start.2 = ((bf16[8,16,1024]{2,1,0:T(8,128)(2,1)}), bf16[8,16,1024]{2,1,0:T(8,128)(2,1)}, u32[]{:S(2)}, u32[]{:S(2)}) async-start(bf16[8,16,1024]{2,1,0:T(8,128)(2,1)} %reshape.99), calls=%async_computation.2 | async-start | bytes 524288 | tf_op jit(solution)/shard_map/all_to_all | solution.py:91
  33.9 1.7 %pad_maximum_fusion = bf16[16,12288]{1,0:T(8,128)(2,1)} fusion(bf16[16,4096]{1,0:T(8,128)(2,1)S(1)} %collective-permute-done.1, bf16[16,4096]{1,0:T(8,128)(2,1)} %param.15, bf16[16,4096]{1,0:T(8,128)(2,1)S(1)} %collective-permute-done), kind=kLoop, calls=%fused_computation.46 | loop fusion | flops 1179648 | bytes 786432 | tf_op jit(solution)/shard_map/concatenate | solution.py:22
  36.5 0.8 gather_fusion.2
  37.3 1.5 %reshape.96 = bf16[8,32,1024]{2,1,0:T(8,128)(2,1)} reshape(bf16[256,16,64]{2,1,0:T(8,128)(2,1)S(1)} %gather_fusion.2) | data formatting | bytes 1048576 | tf_op jit(solution)/shard_map/reshape | solution.py:88
  41.9 1.1 pad_maximum_fusion.1
  43.0 6.0 %all-to-all-start.1 = ((bf16[8,32,1024]{2,1,0:T(8,128)(2,1)}), bf16[8,32,1024]{2,1,0:T(8,128)(2,1)S(1)}, u32[]{:S(2)}, u32[]{:S(2)}) async-start(bf16[8,32,1024]{2,1,0:T(8,128)(2,1)} %reshape.96), calls=%async_computation.1 | async-start | bytes 1048576 | tf_op jit(solution)/shard_map/all_to_all | solution.py:90
  49.0 1.3 reshape.100
  50.3 1.6 %gather_fusion.5 = bf16[128,16,64]{2,1,0:T(8,128)(2,1)} fusion(bf16[128,16,64]{2,1,0:T(8,128)(2,1)S(1)} %reshape.100, s32[1024]{0:T(1024)} %pad_clamp_fusion.1), kind=kCustom, calls=%fused_computation.5 | custom fusion | bytes 524800 | tf_op jit(solution)/shard_map/gather | solution.py:36
  51.9 4.9 %all-gather.2.cloned.1.call-done = bf16[64,12288]{1,0:T(8,128)(2,1)} async-done(((bf16[16,12288]{1,0:T(8,128)(2,1)}), bf16[64,12288]{1,0:T(8,128)(2,1)}) %all-gather.2.cloned.1.call-update) | async-done | bytes 1572880 | tf_op jit(solution)/shard_map/all_gather | solution.py:94
  56.8 2.8 %copy.65 = bf16[8,48,8,256]{3,2,0,1:T(8,128)(2,1)} copy(bf16[8,48,8,256]{3,2,1,0:T(8,128)(2,1)} %bitcast.134) | data formatting | bytes 3145728 | tf_op jit(solution)/shard_map/reshape | solution.py:95
  59.6 63.8 %while.10 = (s32[]{:T(128)}, bf16[4,64,256]{2,0,1:T(4,128)(2,1)}, s32[4]{0:T(128)}, s32[16,16]{1,0:T(8,128)}, bf16[64,48,256]{2,0,1:T(8,128)(2,1)}, /*index=5*/f...) while((s32[]{:T(128)}, bf16[4,64,256]{2,0,1:T(4,128)(2,1)}, ...), condition=%wide.region_1.2_spmd, body=%wide.region_0.1_spmd.sunk | while | flops 147084432 | bytes 2504451 | solution.py:50
  59.6 1.2 dynamic_slice.21
  65.5 1.3 constant_dynamic-slice_fusion.5
  67.5 2.1 %gather_fusion.1 = bf16[16,64,256]{2,1,0:T(8,128)(2,1)S(1)} fusion(bf16[64,48,256]{2,0,1:T(8,128)(2,1)} %get-tuple-element.175, s32[1024]{0:T(1024)} %copy-done.4), kind=kCustom, calls=%fused_computation.clone.1 | custom fusion | bytes 1048640 | tf_op jit(solution)/shard_map/while/body/eval_jaxpr/jit(_take)/gather | solution.py:45
  69.6 3.7 %fusion.38 = bf16[1,64,256]{2,1,0:T(8,128)(2,1)S(1)} fusion(f32[16,256]{1,0:T(8,128)} %get-tuple-element.137, f32[16,256]{1,0:T(8,128)} %get-tuple-element.138, f32[256]{0:T(256)} %bitcast.151, f32[16,256]{1,0:T(8,128)} %get-tuple-element.142, f32[256]{0:T(256)} %bitcast.150, f32[16,256]{1,0:T(8,128)} %get-tuple-element.144, f32[256]{0:T(256)} %bitcast.149, ...), kind=kOutput, calls=%fused_computation.8.clone.1 | convolution fusion | flops 147062784 | bytes 642064 | tf_op jit(solution)/shard_map/while/body/eval_jaxpr/npq,vnq->vp/dot_general | solution.py:48
  73.3 2.3 %dynamic_update_slice.5 = bf16[4,64,256]{2,0,1:T(4,128)(2,1)} dynamic-update-slice(bf16[4,64,256]{2,0,1:T(4,128)(2,1)} %get-tuple-element.160, bf16[1,64,256]{2,0,1:T(2,128)(2,1)S(1)} %copy.74, s32[]{:T(128)S(6)} %copy.78, s32[]{:T(128)} %constant.34.clone.1..sunk, s32[]{:T(128)} %constant.34.clone.1..sunk) | dynamic-update-slice | bytes 65540 | tf_op jit(solution)/shard_map/while/body/jit(dynamic_update_index_in_dim)/dynamic_update_slice | solution.py:50
  75.6 1.2 dynamic_slice.21
  80.0 0.7 compare_and_fusion.2
  81.5 1.3 constant_dynamic-slice_fusion.5
  83.4 2.1 %gather_fusion.1 = bf16[16,64,256]{2,1,0:T(8,128)(2,1)S(1)} fusion(bf16[64,48,256]{2,0,1:T(8,128)(2,1)} %get-tuple-element.175, s32[1024]{0:T(1024)} %copy-done.4), kind=kCustom, calls=%fused_computation.clone.1 | custom fusion | bytes 1048640 | tf_op jit(solution)/shard_map/while/body/eval_jaxpr/jit(_take)/gather | solution.py:45
  85.5 3.7 %fusion.38 = bf16[1,64,256]{2,1,0:T(8,128)(2,1)S(1)} fusion(f32[16,256]{1,0:T(8,128)} %get-tuple-element.137, f32[16,256]{1,0:T(8,128)} %get-tuple-element.138, f32[256]{0:T(256)} %bitcast.151, f32[16,256]{1,0:T(8,128)} %get-tuple-element.142, f32[256]{0:T(256)} %bitcast.150, f32[16,256]{1,0:T(8,128)} %get-tuple-element.144, f32[256]{0:T(256)} %bitcast.149, ...), kind=kOutput, calls=%fused_computation.8.clone.1 | convolution fusion | flops 147062784 | bytes 642064 | tf_op jit(solution)/shard_map/while/body/eval_jaxpr/npq,vnq->vp/dot_general | solution.py:48
  89.3 2.3 %dynamic_update_slice.5 = bf16[4,64,256]{2,0,1:T(4,128)(2,1)} dynamic-update-slice(bf16[4,64,256]{2,0,1:T(4,128)(2,1)} %get-tuple-element.160, bf16[1,64,256]{2,0,1:T(2,128)(2,1)S(1)} %copy.74, s32[]{:T(128)S(6)} %copy.78, s32[]{:T(128)} %constant.34.clone.1..sunk, s32[]{:T(128)} %constant.34.clone.1..sunk) | dynamic-update-slice | bytes 65540 | tf_op jit(solution)/shard_map/while/body/jit(dynamic_update_index_in_dim)/dynamic_update_slice | solution.py:50
  91.5 1.2 dynamic_slice.21
  97.4 1.3 constant_dynamic-slice_fusion.5
  99.4 2.1 %gather_fusion.1 = bf16[16,64,256]{2,1,0:T(8,128)(2,1)S(1)} fusion(bf16[64,48,256]{2,0,1:T(8,128)(2,1)} %get-tuple-element.175, s32[1024]{0:T(1024)} %copy-done.4), kind=kCustom, calls=%fused_computation.clone.1 | custom fusion | bytes 1048640 | tf_op jit(solution)/shard_map/while/body/eval_jaxpr/jit(_take)/gather | solution.py:45
  101.5 3.7 %fusion.38 = bf16[1,64,256]{2,1,0:T(8,128)(2,1)S(1)} fusion(f32[16,256]{1,0:T(8,128)} %get-tuple-element.137, f32[16,256]{1,0:T(8,128)} %get-tuple-element.138, f32[256]{0:T(256)} %bitcast.151, f32[16,256]{1,0:T(8,128)} %get-tuple-element.142, f32[256]{0:T(256)} %bitcast.150, f32[16,256]{1,0:T(8,128)} %get-tuple-element.144, f32[256]{0:T(256)} %bitcast.149, ...), kind=kOutput, calls=%fused_computation.8.clone.1 | convolution fusion | flops 147062784 | bytes 642064 | tf_op jit(solution)/shard_map/while/body/eval_jaxpr/npq,vnq->vp/dot_general | solution.py:48
  105.2 2.3 %dynamic_update_slice.5 = bf16[4,64,256]{2,0,1:T(4,128)(2,1)} dynamic-update-slice(bf16[4,64,256]{2,0,1:T(4,128)(2,1)} %get-tuple-element.160, bf16[1,64,256]{2,0,1:T(2,128)(2,1)S(1)} %copy.74, s32[]{:T(128)S(6)} %copy.78, s32[]{:T(128)} %constant.34.clone.1..sunk, s32[]{:T(128)} %constant.34.clone.1..sunk) | dynamic-update-slice | bytes 65540 | tf_op jit(solution)/shard_map/while/body/jit(dynamic_update_index_in_dim)/dynamic_update_slice | solution.py:50
  107.5 1.2 dynamic_slice.21
  113.4 1.3 constant_dynamic-slice_fusion.5
  115.3 2.1 %gather_fusion.1 = bf16[16,64,256]{2,1,0:T(8,128)(2,1)S(1)} fusion(bf16[64,48,256]{2,0,1:T(8,128)(2,1)} %get-tuple-element.175, s32[1024]{0:T(1024)} %copy-done.4), kind=kCustom, calls=%fused_computation.clone.1 | custom fusion | bytes 1048640 | tf_op jit(solution)/shard_map/while/body/eval_jaxpr/jit(_take)/gather | solution.py:45
  117.4 3.7 %fusion.38 = bf16[1,64,256]{2,1,0:T(8,128)(2,1)S(1)} fusion(f32[16,256]{1,0:T(8,128)} %get-tuple-element.137, f32[16,256]{1,0:T(8,128)} %get-tuple-element.138, f32[256]{0:T(256)} %bitcast.151, f32[16,256]{1,0:T(8,128)} %get-tuple-element.142, f32[256]{0:T(256)} %bitcast.150, f32[16,256]{1,0:T(8,128)} %get-tuple-element.144, f32[256]{0:T(256)} %bitcast.149, ...), kind=kOutput, calls=%fused_computation.8.clone.1 | convolution fusion | flops 147062784 | bytes 642064 | tf_op jit(solution)/shard_map/while/body/eval_jaxpr/npq,vnq->vp/dot_general | solution.py:48
  121.2 2.3 %dynamic_update_slice.5 = bf16[4,64,256]{2,0,1:T(4,128)(2,1)} dynamic-update-slice(bf16[4,64,256]{2,0,1:T(4,128)(2,1)} %get-tuple-element.160, bf16[1,64,256]{2,0,1:T(2,128)(2,1)S(1)} %copy.74, s32[]{:T(128)S(6)} %copy.78, s32[]{:T(128)} %constant.34.clone.1..sunk, s32[]{:T(128)} %constant.34.clone.1..sunk) | dynamic-update-slice | bytes 65540 | tf_op jit(solution)/shard_map/while/body/jit(dynamic_update_index_in_dim)/dynamic_update_slice | solution.py:50
  123.5 3.3 %all-to-all-start = ((bf16[4,64,256]{2,0,1:T(4,128)(2,1)}), bf16[4,64,256]{2,0,1:T(4,128)(2,1)S(1)}, u32[]{:S(2)}, u32[]{:S(2)}) async-start(bf16[4,64,256]{2,0,1:T(4,128)(2,1)} %get-tuple-element.39), calls=%async_computation | async-start | bytes 262144 | tf_op jit(solution)/shard_map/all_to_all | solution.py:99
  126.8 1.9 %fusion.15 = f32[8,16,2,64]{3,1,2,0:T(8,128)S(1)} fusion(bf16[8,2,64,64]{3,2,1,0:T(8,128)(2,1)} %param.20, bf16[8,16,16,64]{3,2,1,0:T(8,128)(2,1)} %bitcast.132, bf16[8,16,64,64]{3,2,1,0:T(8,128)(2,1)S(1)} %copy-done), kind=kOutput, calls=%fused_computation.43 | convolution fusion | flops 18882560 | bytes 1507328 | tf_op jit(solution)/shard_map/mskl,mvl->msvk/dot_general | solution.py:106
  128.8 1.8 %reshape.97 = bf16[256,16,64]{2,1,0:T(8,128)(2,1)S(1)} reshape(bf16[8,32,1024]{2,1,0:T(8,128)(2,1)} %copy-done.1) | data formatting | bytes 1048576 | tf_op jit(solution)/shard_map/reshape | solution.py:35
  130.6 1.8 %gather_fusion.3 = bf16[256,16,64]{2,1,0:T(8,128)(2,1)} fusion(bf16[256,16,64]{2,1,0:T(8,128)(2,1)S(1)} %reshape.97, s32[1024]{0:T(1024)S(1)} %copy-done.7), kind=kCustom, calls=%fused_computation.3 | custom fusion | bytes 1049600 | tf_op jit(solution)/shard_map/gather | solution.py:36
  132.4 3.9 %fusion.9 = bf16[16,16,256]{2,1,0:T(8,128)(2,1)S(1)} fusion(f32[16,16,256]{2,1,0:T(8,128)S(1)} %bitcast.136, bf16[16,64,256]{2,1,0:T(8,128)(2,1)} %param.19, f32[16,16,64]{2,1,0:T(8,128)S(1)} %bitcast.138, bf16[16,16,16,64]{3,2,1,0:T(8,128)(2,1)} %bitcast.130, bf16[16,16,64,64]{3,2,1,0:T(8,128)(2,1)} %param.21), kind=kOutput, calls=%fused_computation.32 | convolution fusion | flops 42106880 | bytes 3604480 | tf_op jit(solution)/shard_map/ikp,ivk->vip/dot_general | solution.py:110
  136.3 7.7 %all_gather.7 = bf16[64,4096]{1,0:T(8,128)(2,1)S(1)} all-gather(bf16[16,4096]{1,0:T(8,128)(2,1)S(1)} %bitcast.139), channel_id=1, replica_groups=mesh['leaf'=8,'vec'=4] {'vec'}, dimensions={0}, use_global_device_ids=true | all-gather | bytes 655360 | tf_op jit(solution)/shard_map/all_gather | solution.py:119
  144.0 0.9 convolution_multiply_fusion
  (102 shorter events, 18.3 us)
Async XLA Ops:
  7.2 119.7 %copy-start = (bf16[8,16,64,64]{3,2,1,0:T(8,128)(2,1)S(1)}, bf16[8,16,64,64]{3,2,1,0:T(8,128)(2,1)}, u32[]{:S(2)}) copy-start(bf16[8,16,64,64]{3,2,1,0:T(8,128)(2,1)} %param.22) | copy-start | bytes 3145732
  7.2 28.5 %copy-start.2 = (f32[3,4096]{1,0:T(4,128)S(1)}, f32[3,4096]{1,0:T(4,128)}, u32[]{:S(2)}) copy-start(f32[3,4096]{1,0:T(4,128)} %param.16) | copy-start | bytes 147460
  7.2 28.4 %copy-start.11 = (s32[8,32]{1,0:T(8,128)S(1)}, s32[8,32]{1,0:T(8,128)}, u32[]{:S(2)}) copy-start(s32[8,32]{1,0:T(8,128)} %param.24) | copy-start | bytes 3076
  7.2 26.7 %collective-permute-start.1 = (bf16[16,4096]{1,0:T(8,128)(2,1)}, bf16[16,4096]{1,0:T(8,128)(2,1)S(1)}, u32[]{:S(2)}, u32[]{:S(2)}) collective-permute-start(bf16[16,4096]{1,0:T(8,128)(2,1)} %param.15), channel_id=1, source_target_pairs={{4,0},{8,4},{12,8},{16,12},{20,16},{24,20},{28,24},{5,1},{9,5},{13... | collective-permute-start | bytes 393224 | tf_op jit(solution)/shard_map/ppermute | solution.py:21
  8.6 25.3 %collective-permute-start = (bf16[16,4096]{1,0:T(8,128)(2,1)}, bf16[16,4096]{1,0:T(8,128)(2,1)S(1)}, u32[]{:S(2)}, u32[]{:S(2)}) collective-permute-start(bf16[16,4096]{1,0:T(8,128)(2,1)} %param.15), channel_id=1, source_target_pairs={{0,4},{4,8},{8,12},{12,16},{16,20},{20,24},{24,28},{1,5},{5,9},{9,... | collective-permute-start | bytes 393224 | tf_op jit(solution)/shard_map/ppermute | solution.py:18
  15.1 26.2 %collective-permute-start.3 = (f32[5,4096]{1,0:T(8,128)S(1)}, f32[5,4096]{1,0:T(8,128)S(1)}, u32[]{:S(2)}, u32[]{:S(2)}) collective-permute-start(f32[5,4096]{1,0:T(8,128)S(1)} %pad_maximum_fusion.2), channel_id=1, source_target_pairs={{4,0},{8,4},{12,8},{16,12},{20,16},{24,20},{28,24},{5,1},{9,5},{13... | collective-permute-start | bytes 245768 | tf_op jit(solution)/shard_map/ppermute | solution.py:21
  16.4 25.5 %collective-permute-start.2 = (f32[5,4096]{1,0:T(8,128)S(1)}, f32[5,4096]{1,0:T(8,128)}, u32[]{:S(2)}, u32[]{:S(2)}) collective-permute-start(f32[5,4096]{1,0:T(8,128)S(1)} %pad_maximum_fusion.2), channel_id=1, source_target_pairs={{0,4},{4,8},{8,12},{12,16},{16,20},{20,24},{24,28},{1,5},{5,9},{9,... | collective-permute-start | bytes 245768 | tf_op jit(solution)/shard_map/ppermute | solution.py:18
  23.3 15.6 %copy-start.9 = (s32[16,16]{1,0:T(8,128)S(1)}, s32[16,16]{1,0:T(8,128)}, u32[]{:S(2)}) copy-start(s32[16,16]{1,0:T(8,128)} %param.26) | copy-start | bytes 3076
  23.3 16.9 %copy-start.10 = (s32[16,16]{1,0:T(8,128)S(1)}, s32[16,16]{1,0:T(8,128)}, u32[]{:S(2)}) copy-start(s32[16,16]{1,0:T(8,128)} %param.23) | copy-start | bytes 3076
  23.3 18.6 %copy-start.6 = (f32[4096]{0:T(1024)S(1)}, f32[4096]{0:T(1024)}, u32[]{:S(2)}) copy-start(f32[4096]{0:T(1024)} %param.18) | copy-start | bytes 49156
  27.6 15.4 %all-to-all-start.2 = ((bf16[8,16,1024]{2,1,0:T(8,128)(2,1)}), bf16[8,16,1024]{2,1,0:T(8,128)(2,1)}, u32[]{:S(2)}, u32[]{:S(2)}) async-start(bf16[8,16,1024]{2,1,0:T(8,128)(2,1)} %reshape.99), calls=%async_computation.2 | async-start | bytes 524288 | tf_op jit(solution)/shard_map/all_to_all | solution.py:91
  33.2 23.6 %all-gather.2.cloned.1.call-start = ((), (), s32[]{:S(2)}) async-start(), calls=%async_computation.3 | async-start | bytes 1966080 | tf_op jit(solution)/shard_map/all_gather | solution.py:94
  41.2 0.7 copy-start.5
  43.0 80.5 %all-to-all-start.1 = ((bf16[8,32,1024]{2,1,0:T(8,128)(2,1)}), bf16[8,32,1024]{2,1,0:T(8,128)(2,1)S(1)}, u32[]{:S(2)}, u32[]{:S(2)}) async-start(bf16[8,32,1024]{2,1,0:T(8,128)(2,1)} %reshape.96), calls=%async_computation.1 | async-start | bytes 1048576 | tf_op jit(solution)/shard_map/all_to_all | solution.py:90
  63.4 4.0 %copy-start.4 = (s32[1024]{0:T(1024)}, s32[1024]{0:T(1024)S(1)}, u32[]{:S(2)}) copy-start(s32[1024]{0:T(1024)S(1)} %pad_clamp_fusion.6) | copy-start | bytes 12292 | tf_op jit(solution)/shard_map/while
  64.7 2.7 %copy-start.8 = (pred[16]{0:T(512)(128)(4,1)}, pred[16]{0:T(512)(128)(4,1)S(1)}, u32[]{:S(2)}) copy-start(pred[16]{0:T(512)(128)(4,1)S(1)} %compare_and_fusion.2) | copy-start | bytes 52 | tf_op jit(solution)/shard_map/while
  79.4 4.0 %copy-start.4 = (s32[1024]{0:T(1024)}, s32[1024]{0:T(1024)S(1)}, u32[]{:S(2)}) copy-start(s32[1024]{0:T(1024)S(1)} %pad_clamp_fusion.6) | copy-start | bytes 12292 | tf_op jit(solution)/shard_map/while
  80.7 2.7 %copy-start.8 = (pred[16]{0:T(512)(128)(4,1)}, pred[16]{0:T(512)(128)(4,1)S(1)}, u32[]{:S(2)}) copy-start(pred[16]{0:T(512)(128)(4,1)S(1)} %compare_and_fusion.2) | copy-start | bytes 52 | tf_op jit(solution)/shard_map/while
  95.4 4.0 %copy-start.4 = (s32[1024]{0:T(1024)}, s32[1024]{0:T(1024)S(1)}, u32[]{:S(2)}) copy-start(s32[1024]{0:T(1024)S(1)} %pad_clamp_fusion.6) | copy-start | bytes 12292 | tf_op jit(solution)/shard_map/while
  96.6 2.7 %copy-start.8 = (pred[16]{0:T(512)(128)(4,1)}, pred[16]{0:T(512)(128)(4,1)S(1)}, u32[]{:S(2)}) copy-start(pred[16]{0:T(512)(128)(4,1)S(1)} %compare_and_fusion.2) | copy-start | bytes 52 | tf_op jit(solution)/shard_map/while
  111.3 4.0 %copy-start.4 = (s32[1024]{0:T(1024)}, s32[1024]{0:T(1024)S(1)}, u32[]{:S(2)}) copy-start(s32[1024]{0:T(1024)S(1)} %pad_clamp_fusion.6) | copy-start | bytes 12292 | tf_op jit(solution)/shard_map/while
  112.6 2.7 %copy-start.8 = (pred[16]{0:T(512)(128)(4,1)}, pred[16]{0:T(512)(128)(4,1)S(1)}, u32[]{:S(2)}) copy-start(pred[16]{0:T(512)(128)(4,1)S(1)} %compare_and_fusion.2) | copy-start | bytes 52 | tf_op jit(solution)/shard_map/while
  123.5 7.1 %copy-start.7 = (s32[1024]{0:T(1024)S(1)}, s32[1024]{0:T(1024)}, u32[]{:S(2)}) copy-start(s32[1024]{0:T(1024)} %pad_clamp_fusion.3) | copy-start | bytes 12292
  123.5 3.4 %copy-start.1 = (bf16[8,32,1024]{2,1,0:T(8,128)(2,1)}, bf16[8,32,1024]{2,1,0:T(8,128)(2,1)S(1)}, u32[]{:S(2)}) copy-start(bf16[8,32,1024]{2,1,0:T(8,128)(2,1)S(1)} %all-to-all-done.1) | copy-start | bytes 1572868
  123.5 8.9 %all-to-all-start = ((bf16[4,64,256]{2,0,1:T(4,128)(2,1)}), bf16[4,64,256]{2,0,1:T(4,128)(2,1)S(1)}, u32[]{:S(2)}, u32[]{:S(2)}) async-start(bf16[4,64,256]{2,0,1:T(4,128)(2,1)} %get-tuple-element.39), calls=%async_computation | async-start | bytes 262144 | tf_op jit(solution)/shard_map/all_to_all | solution.py:99
  136.3 8.6 %copy-start.3 = (bf16[16,2,8,256]{3,2,0,1:T(8,128)(2,1)}, bf16[16,2,8,256]{3,2,0,1:T(8,128)(2,1)S(1)}, u32[]{:S(2)}) copy-start(bf16[16,2,8,256]{3,2,0,1:T(8,128)(2,1)S(1)} %copy.47) | copy-start | bytes 393220
Sparse Core Ops, SparseCore 0:
  35.8 21.0 all-gather.1
where the time goes:
time: 154 us; the launch traced here: 152 us
  local copies, waits for them, and re-layouts  50.2 us (33%)
  starting transfers between devices  29.2 us (19%)
  matrix products  24.1 us (16%)
  between operations  14.3 us (9%)
  other arithmetic  13.3 us (9%)
  loops' own time  8.01 us (5%)
  blocking collectives  7.65 us (5%)
  waiting for transfers between devices  4.94 us (3%)
    dot_general x4, matrix products, one_leaf(): jnp.einsum('npq,vnq->vp', blocks, src_vec, preferred_element_type=jnp.flo...  14.7 us
    ppermute x2, starting transfers between devices, extended(): lax.ppermute(lax.slice_in_dim(block, block.shape[dim] - width, None, axis...  11.6 us
    dynamic_update_slice x8, local copies, waits for them, and re-layouts, near_leaves(): return lax.map(one_leaf, leaf_ids)  9.24 us
    gather x4, local copies, waits for them, and re-layouts, one_leaf(): src_vec = jnp.take(vec_leaves, chosen, axis=1)  8.44 us
    another operation x1, loops' own time, near_leaves(): return lax.map(one_leaf, leaf_ids)  8.01 us
    all_gather x1, blocking collectives, per_device(): shard_rows = lax.all_gather(sample_out, 'vec', axis=0, tiled=True)  7.65 us
    all_to_all x1, starting transfers between devices, per_device(): lax.all_to_all(send_leafs, 'leaf', split_axis=0, concat_axis=0, tiled=True)  5.98 us
    all_to_all x1, starting transfers between devices, per_device(): lax.all_to_all(send_parents, 'leaf', split_axis=0, concat_axis=0, tiled=T...  5.57 us
  transfers between devices with their start and end apart: 8, of which 1 were waited for; matrix products, arithmetic and copies ran while one was open for 54% of the time, Pallas kernels for 0%

commit v1 on v0

v1 whole, which is shorter than its diff:
```python
import functools
import jax
import jax.numpy as jnp
from jax import lax
from jax.experimental import pallas as pl
from jax.experimental.pallas import tpu as pltpu
from jax.sharding import PartitionSpec as P

four_pi = 4.0 * 3.141592653589793
NT = (((1,), (1,)), ((), ()))


def pieces(block):
    first = block.astype(jnp.bfloat16).astype(jnp.float32)
    rest = block - first
    second = rest.astype(jnp.bfloat16).astype(jnp.float32)
    return first, second, rest - second


def main_kernel(
    devices, leaf_dev, leaf_pts, cap0, cap1,
    near_ref, farf_ref, farc_ref, sendf_ref, sendc_ref,
    geo_ref, vec_ref, fine_ref, coarse_ref, cf_ref, cc_ref, transfer_ref, basis_ref,
    out_ref, yfeat, xfeat,
):
    parents = leaf_dev // 2
    nb = farf_ref.shape[0] // leaf_dev
    nbc = farc_ref.shape[0] // parents
    nn = near_ref.shape[0] // leaf_dev

    def make_source(leaf, carry):
        y1, y2, y3 = pieces(geo_ref[leaf])
        rows = jnp.concatenate([y1, y1, y1, y2, y2, y3], axis=0)
        yfeat[leaf] = rows.T.astype(jnp.bfloat16)
        return carry

    lax.fori_loop(0, 3 * leaf_dev, make_source, 0)

    def make_target(leaf, carry):
        geo = geo_ref[leaf_dev + leaf]
        xyz = geo[0:3]
        norm = jnp.sum(xyz * xyz, axis=0, keepdims=True)
        one = jnp.ones_like(norm)
        x8 = jnp.concatenate([-2.0 * xyz, one, norm, jnp.zeros_like(xyz)], axis=0)
        x1, x2, x3 = pieces(x8)
        xfeat[leaf] = jnp.concatenate([x1, x2, x3, x1, x2, x1], axis=0).astype(jnp.bfloat16)
        return carry

    lax.fori_loop(0, leaf_dev, make_target, 0)

    def near_sum(leaf):
        target = xfeat[leaf]

        def step(group, total):
            for lane in range(4):
                chosen = near_ref[leaf * nn + group * 4 + lane]
                dist = jnp.dot(yfeat[chosen], target, preferred_element_type=jnp.float32)
                block = lax.rsqrt(dist.astype(jnp.bfloat16))
                total = total + jnp.dot(vec_ref[chosen], block, preferred_element_type=jnp.float32)
            return total

        zero = jnp.zeros((vec_ref.shape[1], leaf_pts), jnp.float32)
        return lax.fori_loop(0, nn // 4, step, zero)

    def nt(a, b):
        return lax.dot_general(a, b, NT, preferred_element_type=jnp.float32)

    def parent(m, carry):
        coarse = None
        for b in range(nbc):
            row = farc_ref[m * nbc + b]
            src = (row // cap1) * parents + sendc_ref[row]
            term = nt(coarse_ref[src], cc_ref[m, b])
            coarse = term if coarse is None else coarse + term
        coarse = coarse.astype(jnp.bfloat16)
        for s in range(2):
            leaf = 2 * m + s
            field = nt(coarse, transfer_ref[m, s])
            for b in range(nb):
                row = farf_ref[leaf * nb + b]
                src = (row // cap0) * leaf_dev + sendf_ref[row]
                field = field + nt(fine_ref[src], cf_ref[leaf, b])
            local = field.astype(jnp.bfloat16)
            far = jnp.dot(local, basis_ref[leaf], preferred_element_type=jnp.float32)
            out_ref[leaf] = (near_sum(leaf) + far).astype(out_ref.dtype)
        return carry

    lax.fori_loop(0, parents, parent, 0)


def per_device(
    samples, coords, panel_area, quad_weight, leaf_basis, transfer,
    coupling_fine, coupling_coarse, near_list, send_fine, send_coarse, far_fine, far_coarse,
):
    vec_dev, points = samples.shape
    leaf_dev, basis_rank, leaf_pts = leaf_basis.shape
    devices = lax.axis_size("leaf")
    device = lax.axis_index("leaf")
    cap0, cap1 = send_fine.shape[1], send_coarse.shape[1]
    norm = jnp.sum(coords * coords, axis=0, keepdims=True) + panel_area[None, :]
    geo = jnp.concatenate(
        [coords, norm, jnp.ones_like(norm), jnp.zeros_like(coords)], axis=0
    ).reshape(8, leaf_dev, leaf_pts).transpose(1, 0, 2)
    weighted = (samples.astype(jnp.float32) * (quad_weight / four_pi)[None, :]).astype(jnp.bfloat16)
    weighted = weighted.reshape(vec_dev, leaf_dev, leaf_pts).transpose(1, 0, 2)
    forward = [(i, i + 1) for i in range(devices - 1)]
    backward = [(i + 1, i) for i in range(devices - 1)]

    def wide(block):
        low = lax.ppermute(block, "leaf", forward)
        high = lax.ppermute(block, "leaf", backward)
        return jnp.concatenate([low, block, high], axis=0)

    geo_wide, vec_wide = wide(geo), wide(weighted)
    window = (near_list - (device * leaf_dev - leaf_dev)).reshape(-1)
    rows = samples.reshape(vec_dev, leaf_dev, leaf_pts)
    fine_coef = jnp.einsum(
        "ikp,vip->ivk", leaf_basis, rows, preferred_element_type=jnp.float32
    ).astype(jnp.bfloat16)
    coarse_coef = jnp.einsum(
        "mskl,msvk->mvl",
        transfer,
        fine_coef.reshape(-1, 2, vec_dev, basis_rank),
        preferred_element_type=jnp.float32,
    ).astype(jnp.bfloat16)
    fine_all = lax.all_gather(fine_coef, "leaf", axis=0, tiled=True)
    coarse_all = lax.all_gather(coarse_coef, "leaf", axis=0, tiled=True)
    send = jnp.concatenate([send_fine, send_coarse], axis=1)
    got = lax.all_to_all(send, "leaf", split_axis=0, concat_axis=0, tiled=True)
    smem = pl.BlockSpec(memory_space=pltpu.SMEM)
    vmem = pl.BlockSpec(memory_space=pltpu.VMEM)
    out = pl.pallas_call(
        functools.partial(main_kernel, devices, leaf_dev, leaf_pts, cap0, cap1),
        out_shape=jax.ShapeDtypeStruct((leaf_dev, vec_dev, leaf_pts), jnp.bfloat16),
        in_specs=[smem] * 5 + [vmem] * 8,
        out_specs=vmem,
        scratch_shapes=[
            pltpu.VMEM((3 * leaf_dev, leaf_pts, 48), jnp.bfloat16),
            pltpu.VMEM((leaf_dev, 48, leaf_pts), jnp.bfloat16),
        ],
        compiler_params=pltpu.CompilerParams(vmem_limit_bytes=56 * 1024 * 1024),
    )(
        window, far_fine.reshape(-1), far_coarse.reshape(-1),
        got[:, :cap0].reshape(-1), got[:, cap0:].reshape(-1),
        geo_wide, vec_wide, fine_all, coarse_all, coupling_fine, coupling_coarse, transfer, leaf_basis,
    )
    gathered = lax.all_gather(out, "vec", axis=1, tiled=True)
    gram = jnp.einsum("ivp,iwp->ivw", out, gathered, preferred_element_type=jnp.float32)
    gram = gram * (1.0 / leaf_pts)
    sample_out = out.transpose(1, 0, 2).reshape(vec_dev, points)
    return sample_out, gram


def solution(mesh):
    return jax.shard_map(
        per_device,
        mesh=mesh,
        in_specs=(
            P("vec", "leaf"), P(None, "leaf"), P("leaf"), P("leaf"),
            P("leaf", None, None), P("leaf", None, None, None),
            P("leaf", None, None, None), P("leaf", None, None, None),
            P("leaf", None), P("leaf", None), P("leaf", None), P("leaf", None), P("leaf", None),
        ),
        out_specs=(P("vec", "leaf"), P("leaf", "vec", None)),
        check_vma=False,
    )
```

time: 154 us -> 171 us (1.11)
  blocking collectives: 7.65 us -> 74.2 us
  Pallas kernels: 0 us -> 57.2 us
  local copies, waits for them, and re-layouts: 50.2 us -> 6.42 us
  matrix products: 24.1 us -> 4.36 us
  between operations: 14.3 us -> 0.71 us
  starting transfers between devices: 29.2 us -> 19.8 us
  loops' own time: 8.01 us -> 0 us
  other arithmetic: 13.3 us -> 7.82 us
  waiting for transfers between devices: 4.94 us -> 0.01 us
    all_gather x1 -> x3, blocking collectives: 7.65 us -> 74.2 us  [the longest x1 34 us: per_device(): fine_all = lax.all_gather(fine_coef, 'leaf', axis=0, tiled=True)]
    pallas_call x0 -> x1, Pallas kernels: none -> 57.2 us  [per_device(): pl.pallas_call(functools.partial(main_kernel, devices, leaf_dev, leaf_pts...]
    dot_general x8 -> x2, matrix products: 22.9 us -> 3.16 us  [the longest x1 1.82 us: per_device(): jnp.einsum('ivp,iwp->ivw', out, gathered, preferred_element_type=jnp.floa...]
    gather x12 -> x0, local copies, waits for them, and re-layouts: 15.6 us -> none  [the longest x4 8.44 us: one_leaf(): src_vec = jnp.take(vec_leaves, chosen, axis=1)]
    dynamic_update_slice x8 -> x0, local copies, waits for them, and re-layouts: 9.24 us -> none  [near_leaves(): return lax.map(one_leaf, leaf_ids)]
    all_to_all x3 -> x1, starting transfers between devices: 14.9 us -> 6.21 us  [per_device(): got = lax.all_to_all(send, 'leaf', split_axis=0, concat_axis=0, tiled=True)]
    another operation x1 -> x0, loops' own time: 8.01 us -> none  [near_leaves(): return lax.map(one_leaf, leaf_ids)]
    slice x8 -> x1, local copies, waits for them, and re-layouts: 5.57 us -> 0.07 us  [per_device(): got[:, cap0:].reshape(-1)]
  transfers between devices with their start and end apart: 8 -> 5, of which waited for: 1 -> 0; matrix products, arithmetic and copies ran while one was open for 54% -> 7% of each run, Pallas kernels for 0% -> 0%
where the time goes in v1:
time: 171 us; the launch traced here: 170 us
  blocking collectives  74.2 us (43%)
  Pallas kernels  57.2 us (33%)
  starting transfers between devices  19.8 us (12%)
  other arithmetic  7.82 us (5%)
  local copies, waits for them, and re-layouts  6.42 us (4%)
  matrix products  4.36 us (3%)
    pallas_call x1, Pallas kernels, per_device(): pl.pallas_call(functools.partial(main_kernel, devices, leaf_dev, leaf_pts...  57.2 us
    all_gather x1, blocking collectives, per_device(): fine_all = lax.all_gather(fine_coef, 'leaf', axis=0, tiled=True)  34 us
    all_gather x1, blocking collectives, per_device(): coarse_all = lax.all_gather(coarse_coef, 'leaf', axis=0, tiled=True)  32.7 us
    ppermute x2, starting transfers between devices, wide(): low = lax.ppermute(block, 'leaf', forward)  11 us
    all_gather x1, blocking collectives, per_device(): gathered = lax.all_gather(out, 'vec', axis=1, tiled=True)  7.39 us
    all_to_all x1, starting transfers between devices, per_device(): got = lax.all_to_all(send, 'leaf', split_axis=0, concat_axis=0, tiled=True)  6.21 us
  transfers between devices with their start and end apart: 5, of which 0 were waited for; matrix products, arithmetic and copies ran while one was open for 7% of the time, Pallas kernels for 0%

profile of v1, /device:TPU:0, one launch (start us, length us, event | category | flops | bytes accessed | tf_op | source)
XLA Modules:
  0.0 170.4 jit_solution(4752040056459952781)
XLA Ops:
  0.6 0.7 broadcast_multiply_fusion
  1.4 0.9 multiply_convert_fusion
  2.3 1.3 collective-permute-start.3
  3.6 5.5 %collective-permute-start.2 = (bf16[16,16,256]{2,1,0:T(8,128)(2,1)S(1)}, bf16[16,16,256]{2,1,0:T(8,128)(2,1)S(1)}, u32[]{:S(2)}, u32[]{:S(2)}) collective-permute-start(bf16[16,16,256]{2,1,0:T(8,128)(2,1)S(1)} %bitcast.38), channel_id=1, source_target_pairs={{0,4},{4,8},{8,12},{12,16},{16,20},{20,24},{24,28},{1,5},{5,9},{9,... | collective-permute-start | bytes 393224 | tf_op jit(solution)/shard_map/ppermute | solution.py:110
  9.1 0.1 pad.9.clone
  9.2 0.1 pad.8.clone
  9.3 0.9 multiply_reduce_fusion
  10.2 0.7 add.5
  10.9 0.9 maximum_bitcast_fusion
  11.8 1.3 collective-permute-start.1
  13.1 5.4 %collective-permute-start = (f32[16,8,256]{2,1,0:T(8,128)S(1)}, f32[16,8,256]{2,1,0:T(8,128)S(1)}, u32[]{:S(2)}, u32[]{:S(2)}) collective-permute-start(f32[16,8,256]{2,1,0:T(8,128)S(1)} %maximum_bitcast_fusion), channel_id=1, source_target_pairs={{0,4},{4,8},{8,12},{12,16},{16,20},{20,24},{24,28},{1,5},{5,9},{9,... | collective-permute-start | bytes 393224 | tf_op jit(solution)/shard_map/ppermute | solution.py:110
  18.6 1.4 pad_add_fusion
  19.9 6.2 %all-to-all-start = ((s32[8,1,48]{2,1,0:T(1,128)}), s32[8,1,48]{2,1,0:T(1,128)S(1)}, u32[]{:S(2)}, u32[]{:S(2)}) async-start(s32[8,1,48]{2,1,0:T(1,128)} %bitcast), calls=%async_computation | async-start | bytes 8192 | tf_op jit(solution)/shard_map/all_to_all | solution.py:129
  26.1 0.7 broadcast_subtract_fusion
  26.8 1.3 convolution_convert_fusion
  28.2 1.2 fusion
  29.4 34.0 %all_gather.9.fine_ref = bf16[128,16,64]{2,1,0:T(8,128)(2,1)} all-gather(bf16[16,16,64]{2,1,0:T(8,128)(2,1)S(1)} %convolution_convert_fusion), channel_id=1, replica_groups=mesh['leaf'=8,'vec'=4] {'leaf'}, dimensions={0}, use_global_device_ids=true | all-gather | bytes 294912 | tf_op jit(solution)/shard_map/all_gather | solution.py:126
  63.4 32.7 %all_gather.10.coarse_ref = bf16[64,16,64]{2,1,0:T(8,128)(2,1)} all-gather(bf16[8,16,64]{2,1,0:T(8,128)(2,1)S(1)} %fusion), channel_id=1, replica_groups=mesh['leaf'=8,'vec'=4] {'leaf'}, dimensions={0}, use_global_device_ids=true | all-gather | bytes 147456 | tf_op jit(solution)/shard_map/all_gather | solution.py:127
  96.2 1.3 reshape.43.farc_ref
  97.5 1.4 reshape.42.farf_ref
  98.8 0.6 reshape.41.near_ref
  99.5 0.0 all-to-all-done
  99.5 0.1 slice.7
  99.6 0.6 reshape.44.sendf_ref
  100.2 0.7 reshape.45.sendc_ref
  100.9 0.0 collective-permute-done.3
  100.9 0.0 collective-permute-done.2
  100.9 0.8 pad_maximum_fusion.1.vec_ref
  101.7 0.0 collective-permute-done.1
  101.7 0.0 collective-permute-done
  101.7 0.8 pad_maximum_fusion.geo_ref
  102.5 57.2 %shard_map.140 = bf16[16,16,256]{2,1,0:T(8,128)(2,1)} custom-call(s32[256]{0:T(256)} %reshape.41.near_ref, s32[256]{0:T(256)} %reshape.42.farf_ref, s32[128]{0:T(128)} %reshape.43.farc_ref, s32[256]{0:T(256)} %reshape.44.sendf_ref, s32[128]{0:T(128)} %reshape.45.sendc_ref, f32[48,8,256]{2,1,0:T(8,128)} %pad_maximum_fusion.geo_ref, ...), custom_call_target="tpu_custom_call" | custom-call | tf_op jit(solution)/shard_map/pallas_call | solution.py:132
  159.7 7.4 %all_gather.11 = bf16[16,64,256]{2,1,0:T(8,128)(2,1)S(1)} all-gather(bf16[16,16,256]{2,1,0:T(8,128)(2,1)} %shard_map.140), channel_id=1, replica_groups=mesh['leaf'=8,'vec'=4] {'vec'}, dimensions={1}, use_global_device_ids=true | all-gather | bytes 655360 | tf_op jit(solution)/shard_map/all_gather | solution.py:147
  167.1 1.6 copy.25
  168.6 1.8 %convolution_multiply_fusion = f32[16,16,64]{2,1,0:T(8,128)} fusion(bf16[16,16,256]{2,1,0:T(8,128)(2,1)} %shard_map.140, bf16[16,64,256]{2,1,0:T(8,128)(2,1)S(1)} %all_gather.11), kind=kOutput, calls=%fused_computation | convolution fusion | flops 8404992 | bytes 720896 | tf_op jit(solution)/shard_map/ivp,iwp->ivw/dot_general | solution.py:148
  (2 shorter events, 0.0 us)
Async XLA Ops:
  2.3 98.6 %collective-permute-start.3 = (bf16[16,16,256]{2,1,0:T(8,128)(2,1)S(1)}, bf16[16,16,256]{2,1,0:T(8,128)(2,1)S(1)}, u32[]{:S(2)}, u32[]{:S(2)}) collective-permute-start(bf16[16,16,256]{2,1,0:T(8,128)(2,1)S(1)} %bitcast.37), channel_id=1, source_target_pairs={{4,0},{8,4},{12,8},{16,12},{20,16},{24,20},{28,24},{5,1},{9,5},{13... | collective-permute-start | bytes 393224 | tf_op jit(solution)/shard_map/ppermute | solution.py:111
  3.6 97.3 %collective-permute-start.2 = (bf16[16,16,256]{2,1,0:T(8,128)(2,1)S(1)}, bf16[16,16,256]{2,1,0:T(8,128)(2,1)S(1)}, u32[]{:S(2)}, u32[]{:S(2)}) collective-permute-start(bf16[16,16,256]{2,1,0:T(8,128)(2,1)S(1)} %bitcast.38), channel_id=1, source_target_pairs={{0,4},{4,8},{8,12},{12,16},{16,20},{20,24},{24,28},{1,5},{5,9},{9,... | collective-permute-start | bytes 393224 | tf_op jit(solution)/shard_map/ppermute | solution.py:110
  11.8 89.9 %collective-permute-start.1 = (f32[16,8,256]{2,1,0:T(8,128)S(1)}, f32[16,8,256]{2,1,0:T(8,128)S(1)}, u32[]{:S(2)}, u32[]{:S(2)}) collective-permute-start(f32[16,8,256]{2,1,0:T(8,128)S(1)} %maximum_bitcast_fusion), channel_id=1, source_target_pairs={{4,0},{8,4},{12,8},{16,12},{20,16},{24,20},{28,24},{5,1},{9,5},{13... | collective-permute-start | bytes 393224 | tf_op jit(solution)/shard_map/ppermute | solution.py:111
  13.1 88.6 %collective-permute-start = (f32[16,8,256]{2,1,0:T(8,128)S(1)}, f32[16,8,256]{2,1,0:T(8,128)S(1)}, u32[]{:S(2)}, u32[]{:S(2)}) collective-permute-start(f32[16,8,256]{2,1,0:T(8,128)S(1)} %maximum_bitcast_fusion), channel_id=1, source_target_pairs={{0,4},{4,8},{8,12},{12,16},{16,20},{20,24},{24,28},{1,5},{5,9},{9,... | collective-permute-start | bytes 393224 | tf_op jit(solution)/shard_map/ppermute | solution.py:110
  19.9 79.5 %all-to-all-start = ((s32[8,1,48]{2,1,0:T(1,128)}), s32[8,1,48]{2,1,0:T(1,128)S(1)}, u32[]{:S(2)}, u32[]{:S(2)}) async-start(s32[8,1,48]{2,1,0:T(1,128)} %bitcast), calls=%async_computation | async-start | bytes 8192 | tf_op jit(solution)/shard_map/all_to_all | solution.py:129

commit v2 on v1

v2 whole, which is shorter than its diff:
```python
import functools
import jax
import jax.numpy as jnp
from jax import lax
from jax.experimental import pallas as pl
from jax.experimental.pallas import tpu as pltpu
from jax.sharding import PartitionSpec as P

four_pi = 4.0 * 3.141592653589793
NT = (((1,), (1,)), ((), ()))
MESH = pl.DeviceIdType.MESH


def pieces(block):
    first = block.astype(jnp.bfloat16).astype(jnp.float32)
    rest = block - first
    second = rest.astype(jnp.bfloat16).astype(jnp.float32)
    return first, second, rest - second


def main_kernel(
    near_ref, farf_ref, farc_ref,
    geo_ref, sam_ref, send_ref, transfer_ref, basis_ref, cf_hbm, cc_hbm,
    out_ref, gram_ref,
    geo_low, geo_high, sam_low, sam_high, fine_all, coarse_all, got, got_smem, cf_ref, cc_ref,
    yfeat, xfeat, wvec, rows_all,
    halo_send, halo_recv, table_send, table_recv, fine_send, fine_recv, coarse_send, coarse_recv,
    rows_send, rows_recv, local_sem,
    *, caps,
):
    cap0, cap1 = caps
    leaf_dev, basis_rank, leaf_pts = basis_ref.shape
    vec_dev = sam_ref.shape[0]
    parents = leaf_dev // 2
    nb = farf_ref.shape[0] // leaf_dev
    nbc = farc_ref.shape[0] // parents
    nn = near_ref.shape[0] // leaf_dev
    devices, vecs = lax.axis_size("leaf"), lax.axis_size("vec")
    me, row = lax.axis_index("leaf"), lax.axis_index("vec")

    def leaf_peer(step):
        return {"leaf": lax.rem(me + step, devices)}

    def vec_peer(step):
        return {"vec": lax.rem(row + step, vecs)}

    def remote(src, dst, send, recv, peer):
        return pltpu.make_async_remote_copy(
            src_ref=src, dst_ref=dst, send_sem=send, recv_sem=recv,
            device_id=peer, device_id_type=MESH,
        )

    def cut(leaf):
        return pl.ds(pl.multiple_of(leaf * leaf_pts, leaf_pts), leaf_pts)

    def nt(a, b):
        return lax.dot_general(a, b, NT, preferred_element_type=jnp.float32)

    load_fine = pltpu.make_async_copy(cf_hbm, cf_ref, local_sem.at[0])
    load_coarse = pltpu.make_async_copy(cc_hbm, cc_ref, local_sem.at[1])
    load_fine.start()
    load_coarse.start()

    barrier = pltpu.get_barrier_semaphore()

    def greet(step, carry):
        pl.semaphore_signal(barrier, inc=1, device_id=leaf_peer(step), device_id_type=MESH)
        return carry

    lax.fori_loop(1, devices, greet, 0)
    for step in range(1, vecs):
        pl.semaphore_signal(barrier, inc=1, device_id=vec_peer(step), device_id_type=MESH)
    pl.semaphore_wait(barrier, devices - 1 + vecs - 1)

    def halos(side, geo_dst, sam_dst):
        peer = leaf_peer(1 if side == 0 else devices - 1)
        return (
            remote(geo_ref, geo_dst, halo_send.at[side, 0], halo_recv.at[side, 0], peer),
            remote(sam_ref, sam_dst, halo_send.at[side, 1], halo_recv.at[side, 1], peer),
        )

    @pl.when(me < devices - 1)
    def _():
        for copy in halos(0, geo_low, sam_low):
            copy.start()

    @pl.when(me > 0)
    def _():
        for copy in halos(1, geo_high, sam_high):
            copy.start()

    def table_copy(step):
        peer = lax.rem(me + step, devices)
        return remote(
            send_ref.at[peer], got.at[me], table_send.at[step], table_recv.at[step], {"leaf": peer}
        )

    def fine_copy(step):
        part = fine_all.at[pl.ds(me * leaf_dev, leaf_dev)]
        return remote(part, part, fine_send.at[step], fine_recv.at[step], leaf_peer(step))

    def coarse_copy(step):
        part = coarse_all.at[pl.ds(me * parents, parents)]
        return remote(part, part, coarse_send.at[step], coarse_recv.at[step], leaf_peer(step))

    def start_table(step, carry):
        table_copy(step).start()
        return carry

    lax.fori_loop(1, devices, start_table, 0)
    got[me] = send_ref[me]

    def fine_row(leaf, carry):
        coef = nt(sam_ref[:, cut(leaf)], basis_ref[leaf])
        fine_all[me * leaf_dev + leaf] = coef.astype(jnp.bfloat16)
        return carry

    lax.fori_loop(0, leaf_dev, fine_row, 0, unroll=4)

    def start_fine(step, carry):
        fine_copy(step).start()
        return carry

    lax.fori_loop(1, devices, start_fine, 0)

    def coarse_row(m, carry):
        child = me * leaf_dev + 2 * m
        coef = jnp.dot(fine_all[child], transfer_ref[m, 0], preferred_element_type=jnp.float32)
        coef += jnp.dot(fine_all[child + 1], transfer_ref[m, 1], preferred_element_type=jnp.float32)
        coarse_all[me * parents + m] = coef.astype(jnp.bfloat16)
        return carry

    lax.fori_loop(0, parents, coarse_row, 0, unroll=2)

    def start_coarse(step, carry):
        coarse_copy(step).start()
        return carry

    lax.fori_loop(1, devices, start_coarse, 0)

    def prepare(part, geo_src, sam_src):
        def source(leaf, carry):
            geo = geo_src[:, cut(leaf)]
            y1, y2, y3 = pieces(geo)
            rows = jnp.concatenate([y1, y1, y1, y2, y2, y3], axis=0)
            yfeat[part * leaf_dev + leaf] = rows.T.astype(jnp.bfloat16)
            scaled = sam_src[:, cut(leaf)].astype(jnp.float32) * geo[5:6]
            wvec[part * leaf_dev + leaf] = scaled.astype(jnp.bfloat16)
            return carry

        lax.fori_loop(0, leaf_dev, source, 0, unroll=4)

    prepare(1, geo_ref, sam_ref)

    def target(leaf, carry):
        xyz = geo_ref[0:3, cut(leaf)]
        norm = jnp.sum(xyz * xyz, axis=0, keepdims=True)
        x8 = jnp.concatenate(
            [-2.0 * xyz, jnp.ones_like(norm), norm, jnp.zeros_like(xyz)], axis=0
        )
        x1, x2, x3 = pieces(x8)
        xfeat[leaf] = jnp.concatenate([x1, x2, x3, x1, x2, x1], axis=0).astype(jnp.bfloat16)
        return carry

    lax.fori_loop(0, leaf_dev, target, 0, unroll=2)

    @pl.when(me > 0)
    def _():
        for copy in halos(0, geo_low, sam_low):
            copy.wait_recv()
        prepare(0, geo_low, sam_low)

    @pl.when(me < devices - 1)
    def _():
        for copy in halos(1, geo_high, sam_high):
            copy.wait_recv()
        prepare(2, geo_high, sam_high)

    def finish(step, carry):
        table_copy(step).wait()
        fine_copy(step).wait()
        coarse_copy(step).wait()
        return carry

    lax.fori_loop(1, devices, finish, 0)
    to_smem = pltpu.make_async_copy(got, got_smem, local_sem.at[2])
    to_smem.start()
    load_fine.wait()
    load_coarse.wait()
    to_smem.wait()

    def near_sum(leaf):
        features = xfeat[leaf]

        def step(group, total):
            for lane in range(4):
                chosen = near_ref[leaf * nn + group * 4 + lane]
                dist = jnp.dot(yfeat[chosen], features, preferred_element_type=jnp.float32)
                block = lax.rsqrt(dist.astype(jnp.bfloat16))
                total = total + jnp.dot(wvec[chosen], block, preferred_element_type=jnp.float32)
            return total

        zero = jnp.zeros((vec_dev, leaf_pts), jnp.float32)
        return lax.fori_loop(0, nn // 4, step, zero)

    def rows_copy(m, step):
        part = rows_all.at[row, :, pl.ds(pl.multiple_of(m * 2 * leaf_pts, 2 * leaf_pts), 2 * leaf_pts)]
        return remote(part, part, rows_send.at[step, m], rows_recv.at[step, m], vec_peer(step))

    def parent(m, carry):
        coarse = None
        for b in range(nbc):
            slot = farc_ref[m * nbc + b]
            source = lax.div(slot, cap1)
            index = source * parents + got_smem[source, 0, cap0 + lax.rem(slot, cap1)]
            term = nt(coarse_all[index], cc_ref[m, b])
            coarse = term if coarse is None else coarse + term
        coarse = coarse.astype(jnp.bfloat16)
        for s in range(2):
            leaf = 2 * m + s
            field = nt(coarse, transfer_ref[m, s])
            for b in range(nb):
                slot = farf_ref[leaf * nb + b]
                source = lax.div(slot, cap0)
                index = source * leaf_dev + got_smem[source, 0, lax.rem(slot, cap0)]
                field = field + nt(fine_all[index], cf_ref[leaf, b])
            local = field.astype(jnp.bfloat16)
            far = jnp.dot(local, basis_ref[leaf], preferred_element_type=jnp.float32)
            result = (near_sum(leaf) + far).astype(out_ref.dtype)
            rows_all[row, :, cut(leaf)] = result
            out_ref[:, cut(leaf)] = result
        for step in range(1, vecs):
            rows_copy(m, step).start()
        return carry

    lax.fori_loop(0, parents, parent, 0)

    @pl.when(me < devices - 1)
    def _():
        for copy in halos(0, geo_low, sam_low):
            copy.wait_send()

    @pl.when(me > 0)
    def _():
        for copy in halos(1, geo_high, sam_high):
            copy.wait_send()

    def gram_pair(m, carry):
        for step in range(1, vecs):
            rows_copy(m, step).wait()
        for s in range(2):
            leaf = 2 * m + s
            everyone = rows_all[:, :, cut(leaf)].reshape(vecs * vec_dev, leaf_pts)
            gram_ref[leaf] = nt(rows_all[row, :, cut(leaf)], everyone) * (1.0 / leaf_pts)
        return carry

    lax.fori_loop(0, parents, gram_pair, 0)


def per_device(
    samples, coords, panel_area, quad_weight, leaf_basis, transfer,
    coupling_fine, coupling_coarse, near_list, send_fine, send_coarse, far_fine, far_coarse,
):
    vec_dev, points = samples.shape
    leaf_dev, basis_rank, leaf_pts = leaf_basis.shape
    parents = leaf_dev // 2
    devices, vecs = lax.axis_size("leaf"), lax.axis_size("vec")
    device = lax.axis_index("leaf")
    caps = (send_fine.shape[1], send_coarse.shape[1])
    norm = jnp.sum(coords * coords, axis=0, keepdims=True) + panel_area[None, :]
    weight = quad_weight[None, :] / four_pi
    geo = jnp.concatenate(
        [coords, norm, jnp.ones_like(norm), weight, jnp.zeros((2, points), jnp.float32)], axis=0
    )
    window = (near_list - (device * leaf_dev - leaf_dev)).reshape(-1)
    send = jnp.concatenate([send_fine, send_coarse], axis=1)
    width = -(-send.shape[1] // 128) * 128
    send = jnp.pad(send, ((0, 0), (0, width - send.shape[1]))).reshape(devices, 1, width)
    smem = pl.BlockSpec(memory_space=pltpu.SMEM)
    vmem = pl.BlockSpec(memory_space=pltpu.VMEM)
    hbm = pl.BlockSpec(memory_space=pl.ANY)
    bf16 = jnp.bfloat16
    dma = pltpu.SemaphoreType.DMA
    sample_out, gram = pl.pallas_call(
        functools.partial(main_kernel, caps=caps),
        out_shape=(
            jax.ShapeDtypeStruct((vec_dev, points), bf16),
            jax.ShapeDtypeStruct((leaf_dev, vec_dev, vecs * vec_dev), jnp.float32),
        ),
        in_specs=[smem] * 3 + [vmem] * 5 + [hbm] * 2,
        out_specs=(vmem, vmem),
        scratch_shapes=[
            pltpu.VMEM(geo.shape, jnp.float32),
            pltpu.VMEM(geo.shape, jnp.float32),
            pltpu.VMEM(samples.shape, bf16),
            pltpu.VMEM(samples.shape, bf16),
            pltpu.VMEM((devices * leaf_dev, vec_dev, basis_rank), bf16),
            pltpu.VMEM((devices * parents, vec_dev, basis_rank), bf16),
            pltpu.VMEM(send.shape, jnp.int32),
            pltpu.SMEM(send.shape, jnp.int32),
            pltpu.VMEM(coupling_fine.shape, bf16),
            pltpu.VMEM(coupling_coarse.shape, bf16),
            pltpu.VMEM((3 * leaf_dev, leaf_pts, 48), bf16),
            pltpu.VMEM((leaf_dev, 48, leaf_pts), bf16),
            pltpu.VMEM((3 * leaf_dev, vec_dev, leaf_pts), bf16),
            pltpu.VMEM((vecs, vec_dev, points), bf16),
            dma((2, 2)), dma((2, 2)),
            dma((devices,)), dma((devices,)),
            dma((devices,)), dma((devices,)),
            dma((devices,)), dma((devices,)),
            dma((vecs, parents)), dma((vecs, parents)),
            dma((3,)),
        ],
        compiler_params=pltpu.CompilerParams(
            vmem_limit_bytes=56 * 1024 * 1024, collective_id=0, has_side_effects=True
        ),
    )(
        window, far_fine.reshape(-1), far_coarse.reshape(-1),
        geo, samples, send, transfer, leaf_basis, coupling_fine, coupling_coarse,
    )
    return sample_out, gram


def solution(mesh):
    return jax.shard_map(
        per_device,
        mesh=mesh,
        in_specs=(
            P("vec", "leaf"), P(None, "leaf"), P("leaf"), P("leaf"),
            P("leaf", None, None), P("leaf", None, None, None),
            P("leaf", None, None, None), P("leaf", None, None, None),
            P("leaf", None), P("leaf", None), P("leaf", None), P("leaf", None), P("leaf", None),
        ),
        out_specs=(P("vec", "leaf"), P("leaf", "vec", None)),
        check_vma=False,
    )
```

time: 171 us -> 97.8 us (0.57)
  blocking collectives: 74.2 us -> 0 us
  Pallas kernels: 57.2 us -> 84.2 us
  starting transfers between devices: 19.8 us -> 0 us
  matrix products: 4.36 us -> 0 us
  other arithmetic: 7.82 us -> 3.8 us
  local copies, waits for them, and re-layouts: 6.42 us -> 8.62 us
    all_gather x3 -> x0, blocking collectives: 74.2 us -> none  [the longest x1 34 us: per_device(): fine_all = lax.all_gather(fine_coef, 'leaf', axis=0, tiled=True)]
    pallas_call x1, Pallas kernels: 57.2 us -> 84.2 us  [per_device(): pl.pallas_call(functools.partial(main_kernel, caps=caps), out_shape=(jax....]
    ppermute x4 -> x0, starting transfers between devices: 13.5 us -> none  [the longest x2 11 us: wide(): low = lax.ppermute(block, 'leaf', forward)]
    all_to_all x1 -> x0, starting transfers between devices: 6.21 us -> none  [per_device(): got = lax.all_to_all(send, 'leaf', split_axis=0, concat_axis=0, tiled=True)]
    dot_general x3 -> x0, matrix products: 4.36 us -> none  [the longest x1 1.82 us: per_device(): jnp.einsum('ivp,iwp->ivw', out, gathered, preferred_element_type=jnp.floa...]
    unnamed x0 -> x2, local copies, waits for them, and re-layouts: none -> 3.14 us
    reshape x4 -> x0, local copies, waits for them, and re-layouts: 2.89 us -> none  [the longest x1 1.57 us: per_device(): sample_out = out.transpose(1, 0, 2).reshape(vec_dev, points)]
  transfers between devices with their start and end apart: 5 -> 0, of which waited for: 0 -> 0; matrix products, arithmetic and copies ran while one was open for 7% -> 0% of each run, Pallas kernels for 0% -> 0%
where the time goes in v2:
time: 97.8 us; the launch traced here: 97.2 us
  Pallas kernels  84.2 us (86%)
  local copies, waits for them, and re-layouts  8.62 us (9%)
  other arithmetic  3.8 us (4%)
    pallas_call x1, Pallas kernels, per_device(): pl.pallas_call(functools.partial(main_kernel, caps=caps), out_shape=(jax....  84.2 us
    unnamed x2, local copies, waits for them, and re-layouts  3.14 us

profile of v2, /device:TPU:0, one launch (start us, length us, event | category | flops | bytes accessed | tf_op | source)
XLA Modules:
  0.0 97.2 jit_solution(9067113120710008359)
XLA Ops:
  0.6 1.2 %reshape.20.farc_ref = s32[128]{0:T(128)} reshape(s32[8,16]{1,0:T(8,128)} %param.25) | data formatting | bytes 1024 | tf_op jit(solution)/shard_map/reshape | solution.py:318
  1.9 1.4 %reshape.19.farf_ref = s32[256]{0:T(256)} reshape(s32[16,16]{1,0:T(8,128)} %param.24) | data formatting | bytes 2048 | tf_op jit(solution)/shard_map/reshape | solution.py:318
  3.2 0.8 pad_add_fusion
  4.0 0.6 pad.4
  4.6 0.7 broadcast_subtract_fusion
  5.3 0.7 reshape.18.near_ref
  6.0 0.7 broadcast_multiply_fusion
  6.7 0.9 multiply_reduce_fusion
  7.6 0.7 add.9
  8.3 1.6 %concatenate.6.geo_ref = f32[8,4096]{1,0:T(8,128)} concatenate(f32[3,4096]{1,0:T(4,128)} %param.14, f32[1,4096]{1,0:T(1,128)S(1)} %bitcast.3, f32[1,4096]{1,0:T(1,128)S(1)} %broadcast_in_dim.4, f32[1,4096]{1,0:T(1,128)S(1)} %bitcast.4, f32[2,4096]{1,0:T(2,128)S(1)} %broadcast_in_dim.10), dimensions={0} | concatenate | bytes 262144 | tf_op jit(solution)/shard_map/concatenate | solution.py:272
  9.9 84.2 %shard_map.140 = (bf16[16,4096]{1,0:T(8,128)(2,1)}, f32[16,16,64]{2,1,0:T(8,128)}) custom-call(s32[256]{0:T(256)} %reshape.18.near_ref, s32[256]{0:T(256)} %reshape.19.farf_ref, s32[128]{0:T(128)} %reshape.20.farc_ref, f32[8,4096]{1,0:T(8,128)} %concatenate.6.geo_ref, bf16[16,4096]{1,0:T(8,128)(2,1)} %sam_ref.1, s32[8,1,128]{2,1,0:T(1,128)} %bitcast.5, ...), custom_call_target="tpu_custom_call" | custom-call | tf_op jit(solution)/shard_map/pallas_call | solution.py:284
  94.1 1.6 %copy.17 = bf16[16,4096]{1,0:T(8,128)(2,1)} copy(bf16[16,4096]{1,0:T(8,128)(2,1)} %get-tuple-element.4) | data formatting | bytes 262144
  95.7 1.6 %copy.18 = f32[16,16,64]{2,1,0:T(8,128)} copy(f32[16,16,64]{2,1,0:T(8,128)} %get-tuple-element.5) | data formatting | bytes 131072
  (2 shorter events, 0.0 us)

commit v3 on v2

--- a/solution.py
+++ b/solution.py
@@ -20,9 +20,9 @@
 
 def main_kernel(
     near_ref, farf_ref, farc_ref,
-    geo_ref, sam_ref, send_ref, transfer_ref, basis_ref, cf_hbm, cc_hbm,
+    coords_ref, area_ref, weight_ref, sam_ref, send_ref, transfer_ref, basis_ref, cf_hbm, cc_hbm,
     out_ref, gram_ref,
-    geo_low, geo_high, sam_low, sam_high, fine_all, coarse_all, got, got_smem, cf_ref, cc_ref,
+    geo_ref, near_all, geo_low, geo_high, sam_low, sam_high, fine_all, coarse_all, got, got_smem, cf_ref, cc_ref,
     yfeat, xfeat, wvec, rows_all,
     halo_send, halo_recv, table_send, table_recv, fine_send, fine_recv, coarse_send, coarse_recv,
     rows_send, rows_recv, local_sem,
@@ -32,9 +32,9 @@
     leaf_dev, basis_rank, leaf_pts = basis_ref.shape
     vec_dev = sam_ref.shape[0]
     parents = leaf_dev // 2
-    nb = farf_ref.shape[0] // leaf_dev
-    nbc = farc_ref.shape[0] // parents
-    nn = near_ref.shape[0] // leaf_dev
+    nb = farf_ref.shape[1]
+    nbc = farc_ref.shape[1]
+    nn = near_ref.shape[1]
     devices, vecs = lax.axis_size("leaf"), lax.axis_size("vec")
     me, row = lax.axis_index("leaf"), lax.axis_index("vec")
 
@@ -61,6 +61,16 @@
     load_fine.start()
     load_coarse.start()
 
+    def geometry(leaf, carry):
+        xyz = coords_ref[:, cut(leaf)]
+        norm = jnp.sum(xyz * xyz, axis=0, keepdims=True) + area_ref[:, cut(leaf)]
+        weight = weight_ref[:, cut(leaf)] * (1.0 / four_pi)
+        geo_ref[:, cut(leaf)] = jnp.concatenate(
+            [xyz, norm, jnp.ones_like(norm), weight, jnp.zeros_like(xyz[:2])], axis=0
+        )
+        return carry
+
+    lax.fori_loop(0, leaf_dev, geometry, 0, unroll=4)
     barrier = pltpu.get_barrier_semaphore()
 
     def greet(step, carry):
@@ -117,12 +127,6 @@
 
     lax.fori_loop(0, leaf_dev, fine_row, 0, unroll=4)
 
-    def start_fine(step, carry):
-        fine_copy(step).start()
-        return carry
-
-    lax.fori_loop(1, devices, start_fine, 0)
-
     def coarse_row(m, carry):
         child = me * leaf_dev + 2 * m
         coef = jnp.dot(fine_all[child], transfer_ref[m, 0], preferred_element_type=jnp.float32)
@@ -131,12 +135,6 @@
         return carry
 
     lax.fori_loop(0, parents, coarse_row, 0, unroll=2)
-
-    def start_coarse(step, carry):
-        coarse_copy(step).start()
-        return carry
-
-    lax.fori_loop(1, devices, start_coarse, 0)
 
     def prepare(part, geo_src, sam_src):
         def source(leaf, carry):
@@ -176,6 +174,39 @@
             copy.wait_recv()
         prepare(2, geo_high, sam_high)
 
+    def start_fine(step, carry):
+        fine_copy(step).start()
+        return carry
+
+    lax.fori_loop(1, devices, start_fine, 0)
+
+    def start_coarse(step, carry):
+        coarse_copy(step).start()
+        return carry
+
+    lax.fori_loop(1, devices, start_coarse, 0)
+
+    def near_sum(leaf):
+        features = xfeat[leaf]
+
+        def step(group, total):
+            for lane in range(4):
+                offset = near_ref[leaf, group * 4 + lane] - (me - 1) * leaf_dev
+                chosen = jnp.clip(offset, 0, 3 * leaf_dev - 1)
+                dist = jnp.dot(yfeat[chosen], features, preferred_element_type=jnp.float32)
+                block = lax.rsqrt(dist.astype(jnp.bfloat16))
+                total = total + jnp.dot(wvec[chosen], block, preferred_element_type=jnp.float32)
+            return total
+
+        zero = jnp.zeros((vec_dev, leaf_pts), jnp.float32)
+        return lax.fori_loop(0, nn // 4, step, zero)
+
+    def near_leaf(leaf, carry):
+        near_all[leaf] = near_sum(leaf)
+        return carry
+
+    lax.fori_loop(0, leaf_dev, near_leaf, 0)
+
     def finish(step, carry):
         table_copy(step).wait()
         fine_copy(step).wait()
@@ -189,20 +220,6 @@
     load_coarse.wait()
     to_smem.wait()
 
-    def near_sum(leaf):
-        features = xfeat[leaf]
-
-        def step(group, total):
-            for lane in range(4):
-                chosen = near_ref[leaf * nn + group * 4 + lane]
-                dist = jnp.dot(yfeat[chosen], features, preferred_element_type=jnp.float32)
-                block = lax.rsqrt(dist.astype(jnp.bfloat16))
-                total = total + jnp.dot(wvec[chosen], block, preferred_element_type=jnp.float32)
-            return total
-
-        zero = jnp.zeros((vec_dev, leaf_pts), jnp.float32)
-        return lax.fori_loop(0, nn // 4, step, zero)
-
     def rows_copy(m, step):
         part = rows_all.at[row, :, pl.ds(pl.multiple_of(m * 2 * leaf_pts, 2 * leaf_pts), 2 * leaf_pts)]
         return remote(part, part, rows_send.at[step, m], rows_recv.at[step, m], vec_peer(step))
@@ -210,7 +227,7 @@
     def parent(m, carry):
         coarse = None
         for b in range(nbc):
-            slot = farc_ref[m * nbc + b]
+            slot = farc_ref[m, b]
             source = lax.div(slot, cap1)
             index = source * parents + got_smem[source, 0, cap0 + lax.rem(slot, cap1)]
             term = nt(coarse_all[index], cc_ref[m, b])
@@ -220,13 +237,13 @@
             leaf = 2 * m + s
             field = nt(coarse, transfer_ref[m, s])
             for b in range(nb):
-                slot = farf_ref[leaf * nb + b]
+                slot = farf_ref[leaf, b]
                 source = lax.div(slot, cap0)
                 index = source * leaf_dev + got_smem[source, 0, lax.rem(slot, cap0)]
                 field = field + nt(fine_all[index], cf_ref[leaf, b])
             local = field.astype(jnp.bfloat16)
             far = jnp.dot(local, basis_ref[leaf], preferred_element_type=jnp.float32)
-            result = (near_sum(leaf) + far).astype(out_ref.dtype)
+            result = (near_all[leaf] + far).astype(out_ref.dtype)
             rows_all[row, :, cut(leaf)] = result
             out_ref[:, cut(leaf)] = result
         for step in range(1, vecs):
@@ -265,14 +282,7 @@
     leaf_dev, basis_rank, leaf_pts = leaf_basis.shape
     parents = leaf_dev // 2
     devices, vecs = lax.axis_size("leaf"), lax.axis_size("vec")
-    device = lax.axis_index("leaf")
     caps = (send_fine.shape[1], send_coarse.shape[1])
-    norm = jnp.sum(coords * coords, axis=0, keepdims=True) + panel_area[None, :]
-    weight = quad_weight[None, :] / four_pi
-    geo = jnp.concatenate(
-        [coords, norm, jnp.ones_like(norm), weight, jnp.zeros((2, points), jnp.float32)], axis=0
-    )
-    window = (near_list - (device * leaf_dev - leaf_dev)).reshape(-1)
     send = jnp.concatenate([send_fine, send_coarse], axis=1)
     width = -(-send.shape[1] // 128) * 128
     send = jnp.pad(send, ((0, 0), (0, width - send.shape[1]))).reshape(devices, 1, width)
@@ -287,11 +297,13 @@
             jax.ShapeDtypeStruct((vec_dev, points), bf16),
             jax.ShapeDtypeStruct((leaf_dev, vec_dev, vecs * vec_dev), jnp.float32),
         ),
-        in_specs=[smem] * 3 + [vmem] * 5 + [hbm] * 2,
+        in_specs=[smem] * 3 + [vmem] * 7 + [hbm] * 2,
         out_specs=(vmem, vmem),
         scratch_shapes=[
-            pltpu.VMEM(geo.shape, jnp.float32),
-            pltpu.VMEM(geo.shape, jnp.float32),
+            pltpu.VMEM((8, points), jnp.float32),
+            pltpu.VMEM((leaf_dev, vec_dev, leaf_pts), jnp.float32),
+            pltpu.VMEM((8, points), jnp.float32),
+            pltpu.VMEM((8, points), jnp.float32),
             pltpu.VMEM(samples.shape, bf16),
             pltpu.VMEM(samples.shape, bf16),
             pltpu.VMEM((devices * leaf_dev, vec_dev, basis_rank), bf16),
@@ -315,8 +327,8 @@
             vmem_limit_bytes=56 * 1024 * 1024, collective_id=0, has_side_effects=True
         ),
     )(
-        window, far_fine.reshape(-1), far_coarse.reshape(-1),
-        geo, samples, send, transfer, leaf_basis, coupling_fine, coupling_coarse,
+        near_list, far_fine, far_coarse,
+        coords, panel_area[None, :], quad_weight[None, :], samples, send, transfer, leaf_basis, coupling_fine, coupling_coarse,
     )
     return sample_out, gram
 

time: 97.8 us -> 78.3 us (0.80)
  the two profiles are of different devices: /device:TPU:0 before, /device:TPU:11 now
where the time goes in v3:
time: 78.3 us; the launch traced here: 78.1 us
  Pallas kernels  73 us (93%)
  local copies, waits for them, and re-layouts  3.73 us (5%)
    pallas_call x1, Pallas kernels, per_device(): pl.pallas_call(functools.partial(main_kernel, caps=caps), out_shape=(jax....  73 us
    unnamed x2, local copies, waits for them, and re-layouts  3.14 us

profile of v3, /device:TPU:11, one launch (start us, length us, event | category | flops | bytes accessed | tf_op | source)
XLA Modules:
  0.0 78.1 jit_solution(2971559526790253481)
XLA Ops:
  0.6 0.8 pad_add_fusion
  1.4 0.6 pad.4
  2.0 73.0 %shard_map.140 = (bf16[16,4096]{1,0:T(8,128)(2,1)}, f32[16,16,64]{2,1,0:T(8,128)}) custom-call(s32[16,16]{1,0:T(8,128)} %near_ref.1, s32[16,16]{1,0:T(8,128)} %farf_ref.1, s32[8,16]{1,0:T(8,128)} %farc_ref.1, f32[3,4096]{1,0:T(4,128)} %coords_ref.1, f32[1,4096]{1,0:T(1,128)} %bitcast.3, f32[1,4096]{1,0:T(1,128)} %bitcast.4, bf16[16,4096]{1,0:T(8,128)(2,1)} %sam_ref.1, ...), custom_call_target="tpu_custom_call" | custom-call | tf_op jit(solution)/shard_map/pallas_call | solution.py:294
  75.0 1.6 %copy.17 = bf16[16,4096]{1,0:T(8,128)(2,1)} copy(bf16[16,4096]{1,0:T(8,128)(2,1)} %get-tuple-element.4) | data formatting | bytes 262144
  76.6 1.6 %copy.18 = f32[16,16,64]{2,1,0:T(8,128)} copy(f32[16,16,64]{2,1,0:T(8,128)} %get-tuple-element.5) | data formatting | bytes 131072
